TPU v7x, 32 devices: a whole 2x2x4 slice. The times are simulated.
32 devices in a mesh: row: 8 (over z, x), col: 4 (over y, core).
Axes of the slice: x: 2, y: 2, z: 4, core: 2. Of those that a mesh axis runs over, the one named last changes fastest.
Arguments:
- matrix: float32 [64, 8, 128, 128], P('row', 'col'), may hold values from -0.1875 to 0.1875
- columns: int32 [64, 8], P('row', 'col'), may hold values from 0 to 15
- counts: int32 [64, 4], P('row', 'col'), may hold values from 1 to 2
- fine_guess: float32 [64, 32, 128], P(('col', 'row')), may hold values from -6 to 6
- right_side: float32 [64, 32, 128], P(('row', 'col')), may hold values from -6 to 6
- aggregate: int32 [64], P(('row', 'col')), may hold values from 0 to 7
- restrict: float32 [64, 128, 128], P(('row', 'col')), may hold values from -0.5 to 0.5
Outputs:
- coarse_scaled: float32 [64, 32, 128], P('row')
- residual: float32 [64, 32, 128], P(('row', 'col'))
Inputs may be any that keep to these rules, and one draw needn't show every extreme that they name: `counts`: slots at or past the count hold no part of the operator.
All inputs are finite; a program needn't handle non-finite values.
Results may differ from a plain program's by a relative error of at most 0.000071.
Values sent between devices are 32-bit elements; how exact they have to be, the bound alone decides.
A program may use at most 64 MiB of HBM per device.

v0:
```python
import jax
import jax.numpy as jnp
from jax import lax
from jax.sharding import PartitionSpec as P

NC_GRP = 8


def local(matrix, columns, counts, fine_guess, right_side, aggregate, restrict):
    column_vector = lax.all_gather(fine_guess, "row", axis=0, tiled=True)
    slot_count = matrix.shape[1]
    usable = jnp.arange(slot_count, dtype=jnp.int32)[None, :] < counts
    picked = jnp.take(column_vector, columns, axis=0) * usable[:, :, None, None].astype(jnp.float32)
    partial_value = jnp.einsum("gsab,gsvb->gva", matrix, picked, precision=lax.Precision.HIGHEST)
    product = lax.psum_scatter(partial_value, "col", scatter_dimension=0, tiled=True)
    residual = right_side - product
    contrib = jnp.einsum("gva,gak->gvk", residual, restrict, precision=lax.Precision.HIGHEST)
    onehot = (aggregate[:, None] == jnp.arange(NC_GRP, dtype=jnp.int32)[None, :]).astype(
        jnp.float32
    )
    coarse_part = jnp.einsum("gc,gvk->cvk", onehot, contrib, precision=lax.Precision.HIGHEST)
    squares = jnp.sum(residual * residual, axis=(0, 2))
    coarse = lax.psum(coarse_part, "col")
    total_sq = lax.psum(squares, ("row", "col"))
    entries = residual.shape[0] * residual.shape[2] * lax.axis_size("row") * lax.axis_size("col")
    scale_rms = jnp.sqrt(total_sq / entries + 1e-06)
    return (coarse / scale_rms[None, :, None], residual)


def solution(mesh):
    in_specs = (
        P("row", "col", None, None),
        P("row", "col"),
        P("row", "col"),
        P(("col", "row"), None, None),
        P(("row", "col"), None, None),
        P(("row", "col")),
        P(("row", "col"), None, None),
    )
    out_specs = (P("row", None, None), P(("row", "col"), None, None))
    return jax.shard_map(local, mesh=mesh, in_specs=in_specs, out_specs=out_specs, check_vma=False)
```

profile of v0, /device:TPU:0, one launch (start us, length us, event | category | flops | bytes accessed | tf_op | source)
XLA Modules:
  0.0 115.5 jit_solution(6656684423005813290)
XLA Ops:
  7.2 0.0 copy-start
  7.2 0.0 copy-start.4
  7.2 0.0 reduce-scatter.2.cloned.1.call-start
  7.2 0.8 compare_select_fusion
  8.0 0.0 copy-done.4
  8.0 32.8 %all_gather.3 = f32[16,32,128]{2,1,0:T(8,128)S(1)} all-gather(f32[2,32,128]{2,1,0:T(8,128)} %param.10), channel_id=1, replica_groups=mesh['row'=8,'col'=4] {'row'}, dimensions={0}, use_global_device_ids=true | all-gather | bytes 294912 | tf_op jit(solution)/shard_map/all_gather | solution.py:10
  40.8 0.1 copy.16
  40.9 0.1 reshape.37
  40.9 0.0 copy-start.6
  41.0 0.6 copy-done.6
  41.6 0.1 fusion.7
  41.7 0.1 copy.15
  41.8 0.6 gather_fusion
  42.3 0.0 copy-done
  42.4 0.0 copy-start.3
  42.4 1.9 %convolution_bitcast_fusion = f32[8,32,128]{2,1,0:T(8,128)} fusion(f32[8,2,128,128]{3,2,1,0:T(8,128)S(1)} %copy-done, f32[8,2,32,128]{3,2,1,0:T(8,128)S(1)} %bitcast.11, f32[8,2]{1,0:T(8,128)S(1)} %fusion.7, pred[8,2]{1,0:T(8,128)(4,1)S(1)} %copy.15), kind=kOutput, calls=%fused_computation.1 | convolution fusion | flops 100794368 | bytes 1441872 | tf_op jit(solution)/shard_map/gsab,gsvb->gva/dot_general | solution.py:14
  44.3 0.0 copy-start.1
  44.3 0.0 reduce-scatter.2.cloned.1.call-update
  44.3 0.0 all-reduce.2.cloned.1.call-start
  44.3 20.7 %reduce-scatter.2.cloned.1.call-done = f32[2,32,128]{2,1,0:T(8,128)} async-done(((f32[8,32,128]{2,1,0:T(8,128)}), f32[2,32,128]{2,1,0:T(8,128)}) %reduce-scatter.2.cloned.1.call-update) | async-done | bytes 32784 | tf_op jit(solution)/shard_map/reduce_scatter | solution.py:15
  65.0 0.0 copy-done.3
  65.0 0.9 multiply_reduce_fusion
  65.9 0.0 copy-start.2
  65.9 0.0 copy-done.1
  65.9 0.0 copy-start.5
  65.9 0.2 fusion.13
  66.2 0.4 copy-done.2
  66.5 0.1 copy-done.5
  66.6 1.0 fusion.5
  67.6 0.0 all-reduce.2.cloned.1.call-update
  67.6 39.3 %psum.15 = f32[32]{0:T(128)S(1)} all-reduce(f32[32]{0:T(128)S(1)} %get-tuple-element.8), channel_id=1, replica_groups=mesh['row'=8,'col'=4] {'row','col'}, use_global_device_ids=true, to_apply=%region_3.4 | all-reduce | flops 32 | bytes 256 | tf_op jit(solution)/shard_map/psum | solution.py:24
  106.9 0.0 all-reduce.2.cloned.1.call-done
  107.0 1.0 broadcast_divide_fusion
  108.0 0.7 copy.18
  (3 shorter events, 0.0 us)
Async XLA Ops:
  7.2 35.2 %copy-start = (f32[8,2,128,128]{3,2,1,0:T(8,128)S(1)}, f32[8,2,128,128]{3,2,1,0:T(8,128)}, u32[]{:S(2)}) copy-start(f32[8,2,128,128]{3,2,1,0:T(8,128)} %param.7) | copy-start | bytes 3145732
  7.2 0.8 copy-start.4
  7.2 57.8 %reduce-scatter.2.cloned.1.call-start = ((), (), s32[]{:S(2)}) async-start(), calls=%async_computation.1 | async-start | bytes 163840 | tf_op jit(solution)/shard_map/reduce_scatter | solution.py:15
  40.9 0.7 copy-start.6
  42.4 22.7 %copy-start.3 = (f32[2,32,128]{2,1,0:T(8,128)S(1)}, f32[2,32,128]{2,1,0:T(8,128)}, u32[]{:S(2)}) copy-start(f32[2,32,128]{2,1,0:T(8,128)} %param.11) | copy-start | bytes 98308
  44.3 21.7 %copy-start.1 = (f32[2,128,128]{2,1,0:T(8,128)S(1)}, f32[2,128,128]{2,1,0:T(8,128)}, u32[]{:S(2)}) copy-start(f32[2,128,128]{2,1,0:T(8,128)} %param.13) | copy-start | bytes 393220
  44.3 62.7 %all-reduce.2.cloned.1.call-start = ((), (), s32[]{:S(2)}) async-start(), calls=%async_computation.2 | async-start | bytes 262144 | tf_op jit(solution)/shard_map/psum | solution.py:23
  65.9 0.6 copy-start.2
  65.9 0.7 copy-start.5
Sparse Core Ops, SparseCore 0:
  44.4 20.5 reduce-scatter.1
  67.9 31.7 all-reduce.1
where the time goes:
time: 116 us; the launch traced here: 115 us
  blocking collectives  72.1 us (62%)
  waiting for transfers between devices  20.8 us (18%)
  between operations  14.1 us (12%)
  matrix products  3.07 us (3%)
  other arithmetic  2.73 us (2%)
  local copies, waits for them, and re-layouts  2.62 us (2%)
    psum x1, blocking collectives, local(): total_sq = lax.psum(squares, ('row', 'col'))  39.3 us
    all_gather x1, blocking collectives, local(): column_vector = lax.all_gather(fine_guess, 'row', axis=0, tiled=True)  32.8 us
    reduce_scatter x1, waiting for transfers between devices, local(): lax.psum_scatter(partial_value, 'col', scatter_dimension=0, tiled=True)  20.7 us
  transfers between devices with their start and end apart: 2, of which 1 were waited for; matrix products, arithmetic and copies ran while one was open for 0% of the time, Pallas kernels for 0%

commit v1 on v0

v1 whole, which is shorter than its diff:
```python
import functools

import jax
import jax.numpy as jnp
from jax import lax
from jax.experimental import pallas as pl
from jax.experimental.pallas import tpu as pltpu
from jax.sharding import PartitionSpec as P

NC_GRP = 8
F32 = jnp.float32
BF16 = jnp.bfloat16


def offsets(count):
    inner = 2 if count % 2 == 0 else 1
    outer = count // inner
    steps = [(o, i) for o in range(outer) for i in range(inner) if (o, i) != (0, 0)]
    steps.sort(key=lambda s: -min(s[0], outer - s[0]))
    return inner, outer, steps


def peer(index, inner, outer, step):
    high = lax.rem(lax.div(index, inner) + step[0], outer)
    low = lax.rem(lax.rem(index, inner) + step[1], inner)
    return high * inner + low


def split(value):
    high = value.astype(BF16)
    return high, (value - high.astype(F32)).astype(BF16)


def dot4(left, right):
    m, n = left.shape[0], right.shape[1] // 2
    both = jnp.concatenate(split(left), axis=0)
    out = jnp.dot(both, right, preferred_element_type=F32)
    return out[:m, :n] + (out[:m, n:] + out[m:, :n]) + out[m:, n:]


def kernel(
    n_row, n_col, columns, counts, aggregate, matrix, guess, right_side, restrict,
    coarse_out, residual_out,
    xbuf, mbuf, wbuf, rbuf, rwbuf, rhs, part, part_in, agg_own, agg_in, con, con_in, sq, sq_in,
    load_sem, mat_sem, zsend, zrecv, xsend, xrecv, psend, precv, asend, arecv, csend, crecv, qsend, qrecv,
):
    row, col = lax.axis_index("row"), lax.axis_index("col")
    n_dev = n_row * n_col
    me = row * n_col + col
    blocks = guess.shape[0]
    own_rows = right_side.shape[0]
    slots = matrix.shape[1]
    nv = guess.shape[1]
    width = matrix.shape[3]
    r_in, r_out, _ = offsets(n_row)
    c_in, c_out, c_steps = offsets(n_col)
    z_steps = sorted(range(1, r_out), key=lambda s: -min(s, r_out - s))
    z_wait = sorted(range(1, r_out), key=lambda s: min(s, r_out - s))
    c_peers = [peer(col, c_in, c_out, s) for s in c_steps]
    z_peers = {s: peer(row, r_in, r_out, (s, 0)) for s in z_steps}
    x_steps = list(range(1, r_in))
    x_peers = {s: peer(row, r_in, r_out, (0, s)) for s in x_steps}

    own_slot = pl.ds(row * blocks, blocks)
    load_guess = pltpu.make_async_copy(guess, xbuf.at[own_slot], load_sem.at[0])
    load_guess.start()
    barrier = pltpu.get_barrier_semaphore()
    for p in list(z_peers.values()) + list(x_peers.values()):
        pl.semaphore_signal(barrier, inc=1, device_id=(p, col), device_id_type=pl.DeviceIdType.MESH)
    for p in c_peers:
        pl.semaphore_signal(barrier, inc=1, device_id=(row, p), device_id_type=pl.DeviceIdType.MESH)
    mat_loads = [pltpu.make_async_copy(matrix.at[g], mbuf.at[g], mat_sem.at[g]) for g in range(matrix.shape[0])]
    for c in mat_loads:
        c.start()
    load_restrict = pltpu.make_async_copy(restrict, rbuf, load_sem.at[1])
    load_restrict.start()
    load_rhs = pltpu.make_async_copy(right_side, rhs, load_sem.at[2])
    load_rhs.start()
    for i in range(own_rows):
        agg_own[i] = jnp.full((8, 128), aggregate[i], jnp.int32).astype(F32)
    load_guess.wait()
    pl.semaphore_wait(barrier, len(z_peers) + len(x_peers) + len(c_peers))

    def remote(src, dst, ssem, rsem, r, c):
        return pltpu.make_async_remote_copy(
            src_ref=src, dst_ref=dst, send_sem=ssem, recv_sem=rsem,
            device_id=(r, c), device_id_type=pl.DeviceIdType.MESH,
        )

    sends = []
    z_copies = {}
    for s in z_steps:
        z_copies[s] = remote(xbuf.at[own_slot], xbuf.at[own_slot], zsend.at[s], zrecv.at[s], z_peers[s], col)
        z_copies[s].start()
    x_copies = []
    for s in x_steps:
        c = remote(xbuf.at[own_slot], xbuf.at[own_slot], xsend.at[s, 0], xrecv.at[s, 0], x_peers[s], col)
        c.start()
        x_copies.append(c)
    a_copies = []
    for k, p in enumerate(c_peers):
        c = remote(agg_own, agg_in.at[k], asend.at[k], arecv.at[k], row, p)
        c.start()
        a_copies.append(c)

    for g in range(matrix.shape[0]):
        mat_loads[g].wait()
        for s in range(slots):
            high, low = split(mbuf[g, s].T)
            wbuf[g, s * width:(s + 1) * width, :width] = high
            wbuf[g, s * width:(s + 1) * width, width:] = low
    load_restrict.wait()
    for i in range(own_rows):
        high, low = split(rbuf[i])
        rwbuf[i, :, :high.shape[1]] = high
        rwbuf[i, :, high.shape[1]:] = low

    for s in z_wait:
        z_copies[s].wait_recv()
        source = peer(row, r_in, r_out, (r_out - s, 0))
        got = pl.ds(source * blocks, blocks)
        for t in x_steps:
            c = remote(xbuf.at[got], xbuf.at[got], xsend.at[t, s], xrecv.at[t, s], x_peers[t], col)
            c.start()
            x_copies.append(c)
    for c in x_copies:
        c.wait_recv()

    def product(g):
        picked = []
        for s in range(slots):
            use = jnp.where(s < counts[0, g], 1.0, 0.0).astype(F32)
            picked.append(xbuf[columns[s, g]] * use)
        return dot4(jnp.concatenate(picked, axis=1), wbuf[g])

    p_copies = []
    for k, p in enumerate(c_peers):
        for i in range(own_rows):
            part[k, i] = product(p * own_rows + i)
        c = remote(part.at[k], part_in.at[k], psend.at[k], precv.at[k], row, p)
        c.start()
        p_copies.append(c)
    load_rhs.wait()
    res = [rhs[i] - product(col * own_rows + i) for i in range(own_rows)]
    for k in reversed(range(len(c_peers))):
        p_copies[k].wait_recv()
        for i in range(own_rows):
            res[i] = res[i] - part_in[k, i]

    squares = res[0] * res[0]
    for i in range(1, own_rows):
        squares = squares + res[i] * res[i]
    eye = lax.broadcasted_iota(jnp.int32, (nv, 128), 0) == lax.broadcasted_iota(jnp.int32, (nv, 128), 1)
    by_v = jnp.sum(squares, axis=1, keepdims=True)
    own_sq = jnp.sum(jnp.where(eye, by_v, 0.0), axis=0, keepdims=True)
    sq[...] = own_sq

    def send_squares(d, carry):
        t = lax.rem(me + d, n_dev)
        remote(sq, sq_in.at[d - 1], qsend, qrecv, lax.div(t, n_col), lax.rem(t, n_col)).start()
        return carry

    lax.fori_loop(1, n_dev, send_squares, 0)

    contrib = []
    for i in range(own_rows):
        contrib.append(dot4(res[i], rwbuf[i]))
        con[i] = contrib[i]
    c_copies = []
    for k, p in enumerate(c_peers):
        c = remote(con, con_in.at[k], csend.at[k], crecv.at[k], row, p)
        c.start()
        c_copies.append(c)
    for i in range(own_rows):
        residual_out[i] = res[i]

    def spread(ids, value, total):
        shaped = value.reshape(nv // 8, 8, value.shape[1])
        return [t + jnp.where(ids == c, 1.0, 0.0)[None] * shaped for c, t in enumerate(total)]

    for i in range(own_rows):
        for c in range(NC_GRP):
            mask = jnp.where(agg_own[i] == c, 1.0, 0.0)[None]
            term = mask * contrib[i].reshape(nv // 8, 8, 128)
            if i == 0:
                coarse_out[c] = term.reshape(nv, 128)
            else:
                coarse_out[c] += term.reshape(nv, 128)
    for c in a_copies:
        c.wait_recv()
    for c in c_copies:
        c.wait_recv()
    for c in range(NC_GRP):
        total = coarse_out[c].reshape(nv // 8, 8, 128)
        for k in range(len(c_peers)):
            for i in range(own_rows):
                mask = jnp.where(agg_in[k, i] == c, 1.0, 0.0)[None]
                total = total + mask * con_in[k, i].reshape(nv // 8, 8, 128)
        coarse_out[c] = total.reshape(nv, 128)

    pltpu.make_async_copy(sq_in, sq_in, qrecv).wait()
    all_sq = own_sq + jnp.sum(sq_in[...], axis=0)
    total_v = jnp.sum(jnp.where(eye, all_sq, 0.0), axis=1, keepdims=True)
    inv = 1.0 / jnp.sqrt(total_v / (n_dev * own_rows * 128) + 1e-06)
    for c in range(NC_GRP):
        coarse_out[c] = coarse_out[c] * inv

    for c in list(z_copies.values()) + x_copies + a_copies + p_copies + c_copies:
        c.wait_send()
    pltpu.make_async_copy(sq_in, sq_in, qsend).wait()


def local(n_row, n_col, matrix, columns, counts, fine_guess, right_side, aggregate, restrict):
    blocks, nv, bs = fine_guess.shape
    rows, slots = matrix.shape[:2]
    own_rows = right_side.shape[0]
    cw = restrict.shape[2]
    nc1 = n_col - 1
    r_in, r_out, _ = offsets(n_row)
    dma = pltpu.SemaphoreType.DMA
    vmem = pl.BlockSpec(memory_space=pltpu.VMEM)
    smem = pl.BlockSpec(memory_space=pltpu.SMEM)
    hbm = pl.BlockSpec(memory_space=pl.ANY)
    return pl.pallas_call(
        functools.partial(kernel, n_row, n_col),
        out_shape=(
            jax.ShapeDtypeStruct((NC_GRP, nv, cw), F32),
            jax.ShapeDtypeStruct(right_side.shape, F32),
        ),
        in_specs=[smem] * 3 + [hbm] * 4,
        out_specs=(vmem, vmem),
        scratch_shapes=[
            pltpu.VMEM((n_row * blocks, nv, bs), F32),
            pltpu.VMEM(matrix.shape, F32),
            pltpu.VMEM((rows, slots * bs, 2 * bs), BF16),
            pltpu.VMEM(restrict.shape, F32),
            pltpu.VMEM((own_rows, bs, 2 * cw), BF16),
            pltpu.VMEM(right_side.shape, F32),
            pltpu.VMEM((nc1, own_rows, nv, bs), F32),
            pltpu.VMEM((nc1, own_rows, nv, bs), F32),
            pltpu.VMEM((own_rows, 8, 128), F32),
            pltpu.VMEM((nc1, own_rows, 8, 128), F32),
            pltpu.VMEM((own_rows, nv, cw), F32),
            pltpu.VMEM((nc1, own_rows, nv, cw), F32),
            pltpu.VMEM((1, 128), F32),
            pltpu.VMEM((n_row * n_col - 1, 1, 128), F32),
            dma((3,)), dma((rows,)),
            dma((r_out,)), dma((r_out,)),
            dma((max(r_in, 2), r_out)), dma((max(r_in, 2), r_out)),
            dma((nc1,)), dma((nc1,)),
            dma((nc1,)), dma((nc1,)),
            dma((nc1,)), dma((nc1,)),
            dma(()), dma(()),
        ],
        compiler_params=pltpu.CompilerParams(collective_id=0, has_side_effects=True),
        name="residual_restrict",
    )(columns.T, counts.T, aggregate, matrix, fine_guess, right_side, restrict)


def solution(mesh):
    in_specs = (
        P("row", "col", None, None),
        P("row", "col"),
        P("row", "col"),
        P(("col", "row"), None, None),
        P(("row", "col"), None, None),
        P(("row", "col")),
        P(("row", "col"), None, None),
    )
    out_specs = (P("row", None, None), P(("row", "col"), None, None))
    body = functools.partial(local, mesh.shape["row"], mesh.shape["col"])
    return jax.shard_map(body, mesh=mesh, in_specs=in_specs, out_specs=out_specs, check_vma=False)
```

time: 116 us -> 25.6 us (0.22)
  blocking collectives: 72.1 us -> 0 us
  Pallas kernels: 0 us -> 22.6 us
  waiting for transfers between devices: 20.8 us -> 0 us
  between operations: 14.1 us -> 0.65 us
  matrix products: 3.07 us -> 0 us
  other arithmetic: 2.73 us -> 0 us
    psum x1 -> x0, blocking collectives: 39.3 us -> none  [local(): total_sq = lax.psum(squares, ('row', 'col'))]
    all_gather x1 -> x0, blocking collectives: 32.8 us -> none  [local(): column_vector = lax.all_gather(fine_guess, 'row', axis=0, tiled=True)]
    pallas_call x0 -> x1, Pallas kernels: none -> 22.6 us  [local(): pl.pallas_call(functools.partial(kernel, n_row, n_col), out_shape=(jax.Sh...]
    reduce_scatter x1 -> x0, waiting for transfers between devices: 20.7 us -> none  [local(): lax.psum_scatter(partial_value, 'col', scatter_dimension=0, tiled=True)]
    dot_general x3 -> x0, matrix products: 3.07 us -> none  [the longest x1 1.88 us: local(): jnp.einsum('gsab,gsvb->gva', matrix, picked, precision=lax.Precision.HIGH...]
  transfers between devices with their start and end apart: 2 -> 0, of which waited for: 1 -> 0; matrix products, arithmetic and copies ran while one was open for 0% -> 0% of each run, Pallas kernels for 0% -> 0%
where the time goes in v1:
time: 25.6 us; the launch traced here: 25.4 us
  Pallas kernels  22.6 us (88%)
  local copies, waits for them, and re-layouts  2.19 us (9%)
  between operations  0.65 us (3%)
    pallas_call x1, Pallas kernels, local(): pl.pallas_call(functools.partial(kernel, n_row, n_col), out_shape=(jax.Sh...  22.6 us
    unnamed x4, local copies, waits for them, and re-layouts  2.19 us

profile of v1, /device:TPU:0, one launch (start us, length us, event | category | flops | bytes accessed | tf_op | source)
XLA Modules:
  0.0 25.4 jit_solution(6962351553534332473)
XLA Ops:
  0.6 22.6 %residual_restrict.1 = (f32[8,32,128]{2,1,0:T(8,128)}, f32[2,32,128]{2,1,0:T(8,128)}) custom-call(s32[2,8]{1,0:T(2,128)} %bitcast.2, s32[1,8]{1,0:T(1,128)} %bitcast.3, s32[2]{0:T(128)} %aggregate.1, f32[8,2,128,128]{3,2,1,0:T(8,128)} %matrix.1, f32[2,32,128]{2,1,0:T(8,128)} %guess.1, f32[2,32,128]{2,1,0:T(8,128)} %right_side.1, f32[2,128,128]{2,1,0:T(8,128)} %restrict.1), custom_call_target="tpu_custom_call" | custom-call | tf_op jit(solution)/shard_map/residual_restrict/pallas_call | solution.py:224
  23.2 0.0 copy-start
  23.2 1.6 %copy.11 = f32[8,32,128]{2,1,0:T(8,128)} copy(f32[8,32,128]{2,1,0:T(8,128)} %get-tuple-element.4) | data formatting | bytes 262144
  24.8 0.0 copy-done
  24.8 0.6 %copy.12 = f32[2,32,128]{2,1,0:T(8,128)} copy(f32[2,32,128]{2,1,0:T(8,128)S(1)} %copy-done) | data formatting | bytes 65536
Async XLA Ops:
  23.2 1.6 %copy-start = (f32[2,32,128]{2,1,0:T(8,128)S(1)}, f32[2,32,128]{2,1,0:T(8,128)}, u32[]{:S(2)}) copy-start(f32[2,32,128]{2,1,0:T(8,128)} %get-tuple-element.5) | copy-start | bytes 98308

commit v2 on v1

--- a/solution.py
+++ b/solution.py
@@ -39,9 +39,9 @@
 
 
 def kernel(
-    n_row, n_col, columns, counts, aggregate, matrix, guess, right_side, restrict,
+    n_row, n_col, columns_hbm, counts_hbm, aggregate_hbm, matrix, guess, right_side, restrict,
     coarse_out, residual_out,
-    xbuf, mbuf, wbuf, rbuf, rwbuf, rhs, part, part_in, agg_own, agg_in, con, con_in, sq, sq_in,
+    columns, counts, aggregate, xbuf, mbuf, wbuf, rbuf, rwbuf, rhs, part, part_in, agg_own, agg_in, con, con_in, sq, sq_in,
     load_sem, mat_sem, zsend, zrecv, xsend, xrecv, psend, precv, asend, arecv, csend, crecv, qsend, qrecv,
 ):
     row, col = lax.axis_index("row"), lax.axis_index("col")
@@ -64,11 +64,15 @@
     own_slot = pl.ds(row * blocks, blocks)
     load_guess = pltpu.make_async_copy(guess, xbuf.at[own_slot], load_sem.at[0])
     load_guess.start()
+    scalars = ((columns_hbm, columns), (counts_hbm, counts), (aggregate_hbm, aggregate))
+    scalar_loads = [pltpu.make_async_copy(a, b, load_sem.at[3 + i]) for i, (a, b) in enumerate(scalars)]
     barrier = pltpu.get_barrier_semaphore()
     for p in list(z_peers.values()) + list(x_peers.values()):
         pl.semaphore_signal(barrier, inc=1, device_id=(p, col), device_id_type=pl.DeviceIdType.MESH)
     for p in c_peers:
         pl.semaphore_signal(barrier, inc=1, device_id=(row, p), device_id_type=pl.DeviceIdType.MESH)
+    for c in reversed(scalar_loads):
+        c.start()
     mat_loads = [pltpu.make_async_copy(matrix.at[g], mbuf.at[g], mat_sem.at[g]) for g in range(matrix.shape[0])]
     for c in mat_loads:
         c.start()
@@ -76,8 +80,6 @@
     load_restrict.start()
     load_rhs = pltpu.make_async_copy(right_side, rhs, load_sem.at[2])
     load_rhs.start()
-    for i in range(own_rows):
-        agg_own[i] = jnp.full((8, 128), aggregate[i], jnp.int32).astype(F32)
     load_guess.wait()
     pl.semaphore_wait(barrier, len(z_peers) + len(x_peers) + len(c_peers))
 
@@ -97,6 +99,9 @@
         c = remote(xbuf.at[own_slot], xbuf.at[own_slot], xsend.at[s, 0], xrecv.at[s, 0], x_peers[s], col)
         c.start()
         x_copies.append(c)
+    scalar_loads[2].wait()
+    for i in range(own_rows):
+        agg_own[i] = jnp.full((8, 128), aggregate[i], jnp.int32).astype(F32)
     a_copies = []
     for k, p in enumerate(c_peers):
         c = remote(agg_own, agg_in.at[k], asend.at[k], arecv.at[k], row, p)
@@ -125,6 +130,9 @@
             x_copies.append(c)
     for c in x_copies:
         c.wait_recv()
+
+    scalar_loads[0].wait()
+    scalar_loads[1].wait()
 
     def product(g):
         picked = []
@@ -219,17 +227,19 @@
     r_in, r_out, _ = offsets(n_row)
     dma = pltpu.SemaphoreType.DMA
     vmem = pl.BlockSpec(memory_space=pltpu.VMEM)
-    smem = pl.BlockSpec(memory_space=pltpu.SMEM)
     hbm = pl.BlockSpec(memory_space=pl.ANY)
     return pl.pallas_call(
         functools.partial(kernel, n_row, n_col),
         out_shape=(
-            jax.ShapeDtypeStruct((NC_GRP, nv, cw), F32),
-            jax.ShapeDtypeStruct(right_side.shape, F32),
+            pltpu.VMEM((NC_GRP, nv, cw), F32),
+            pltpu.VMEM(right_side.shape, F32),
         ),
-        in_specs=[smem] * 3 + [hbm] * 4,
+        in_specs=[hbm] * 7,
         out_specs=(vmem, vmem),
         scratch_shapes=[
+            pltpu.SMEM((slots, rows), jnp.int32),
+            pltpu.SMEM((1, rows), jnp.int32),
+            pltpu.SMEM((own_rows,), jnp.int32),
             pltpu.VMEM((n_row * blocks, nv, bs), F32),
             pltpu.VMEM(matrix.shape, F32),
             pltpu.VMEM((rows, slots * bs, 2 * bs), BF16),
@@ -244,7 +254,7 @@
             pltpu.VMEM((nc1, own_rows, nv, cw), F32),
             pltpu.VMEM((1, 128), F32),
             pltpu.VMEM((n_row * n_col - 1, 1, 128), F32),
-            dma((3,)), dma((rows,)),
+            dma((6,)), dma((rows,)),
             dma((r_out,)), dma((r_out,)),
             dma((max(r_in, 2), r_out)), dma((max(r_in, 2), r_out)),
             dma((nc1,)), dma((nc1,)),

time: 25.6 us -> 23.3 us (0.910)
  Pallas kernels: 22.6 us -> 21.3 us
  local copies, waits for them, and re-layouts: 2.19 us -> 1.27 us
    pallas_call x1, Pallas kernels: 22.6 us -> 21.3 us  [local(): pl.pallas_call(functools.partial(kernel, n_row, n_col), out_shape=(pltpu....]
    unnamed x4 -> x2, local copies, waits for them, and re-layouts: 2.19 us -> 1.27 us
where the time goes in v2:
time: 23.3 us; the launch traced here: 23.2 us
  Pallas kernels  21.3 us (91%)
  local copies, waits for them, and re-layouts  1.27 us (5%)
  between operations  0.64 us (3%)
    pallas_call x1, Pallas kernels, local(): pl.pallas_call(functools.partial(kernel, n_row, n_col), out_shape=(pltpu....  21.3 us
    unnamed x2, local copies, waits for them, and re-layouts  1.27 us

profile of v2, /device:TPU:0, one launch (start us, length us, event | category | flops | bytes accessed | tf_op | source)
XLA Modules:
  0.0 23.2 jit_solution(920211341400942346)
XLA Ops:
  0.6 21.3 %residual_restrict.1 = (f32[8,32,128]{2,1,0:T(8,128)S(1)}, f32[2,32,128]{2,1,0:T(8,128)S(1)}) custom-call(s32[2,8]{1,0:T(2,128)} %bitcast.2, s32[1,8]{1,0:T(1,128)} %bitcast.3, s32[2]{0:T(128)} %aggregate_hbm.1, f32[8,2,128,128]{3,2,1,0:T(8,128)} %matrix.1, f32[2,32,128]{2,1,0:T(8,128)} %guess.1, f32[2,32,128]{2,1,0:T(8,128)} %right_side.1, ...), custom_call_target="tpu_custom_call" | custom-call | tf_op jit(solution)/shard_map/residual_restrict/pallas_call | solution.py:231
  21.9 0.7 %copy.11 = f32[8,32,128]{2,1,0:T(8,128)} copy(f32[8,32,128]{2,1,0:T(8,128)S(1)} %get-tuple-element.2) | data formatting | bytes 262144
  22.6 0.6 %copy.12 = f32[2,32,128]{2,1,0:T(8,128)} copy(f32[2,32,128]{2,1,0:T(8,128)S(1)} %get-tuple-element.3) | data formatting | bytes 65536

commit v3 on v2

--- a/solution.py
+++ b/solution.py
@@ -23,6 +23,23 @@
 def peer(index, inner, outer, step):
     high = lax.rem(lax.div(index, inner) + step[0], outer)
     low = lax.rem(lax.rem(index, inner) + step[1], inner)
+    return high * inner + low
+
+
+def swap(index, step, count):
+    out, bit = 0, 1
+    while bit < count:
+        out = out + lax.rem(lax.div(index, bit) + (step // bit) % 2, 2) * bit
+        bit *= 2
+    return out
+
+
+def row_peer(row, inner, outer, step, back=False):
+    low = lax.rem(lax.rem(row, inner) + step[1], inner)
+    if outer & (outer - 1):
+        high = lax.rem(lax.div(row, inner) + (outer - step[0] if back else step[0]), outer)
+    else:
+        high = swap(lax.div(row, inner), step[0], outer)
     return high * inner + low
 
 
@@ -54,12 +71,12 @@
     width = matrix.shape[3]
     r_in, r_out, _ = offsets(n_row)
     c_in, c_out, c_steps = offsets(n_col)
-    z_steps = sorted(range(1, r_out), key=lambda s: -min(s, r_out - s))
-    z_wait = sorted(range(1, r_out), key=lambda s: min(s, r_out - s))
+    z_wait = list(range(1, r_out))
+    z_steps = z_wait[1:] + z_wait[:1]
     c_peers = [peer(col, c_in, c_out, s) for s in c_steps]
-    z_peers = {s: peer(row, r_in, r_out, (s, 0)) for s in z_steps}
+    z_peers = {s: row_peer(row, r_in, r_out, (s, 0)) for s in z_steps}
     x_steps = list(range(1, r_in))
-    x_peers = {s: peer(row, r_in, r_out, (0, s)) for s in x_steps}
+    x_peers = {s: row_peer(row, r_in, r_out, (0, s)) for s in x_steps}
 
     own_slot = pl.ds(row * blocks, blocks)
     load_guess = pltpu.make_async_copy(guess, xbuf.at[own_slot], load_sem.at[0])
@@ -122,7 +139,7 @@
 
     for s in z_wait:
         z_copies[s].wait_recv()
-        source = peer(row, r_in, r_out, (r_out - s, 0))
+        source = row_peer(row, r_in, r_out, (s, 0), back=True)
         got = pl.ds(source * blocks, blocks)
         for t in x_steps:
             c = remote(xbuf.at[got], xbuf.at[got], xsend.at[t, s], xrecv.at[t, s], x_peers[t], col)

time: 23.3 us -> 22.6 us (0.970)
  Pallas kernels: 21.3 us -> 20.6 us
    pallas_call x1, Pallas kernels: 21.3 us -> 20.6 us  [local(): pl.pallas_call(functools.partial(kernel, n_row, n_col), out_shape=(pltpu....]
where the time goes in v3:
time: 22.6 us; the launch traced here: 22.5 us
  Pallas kernels  20.6 us (91%)
  local copies, waits for them, and re-layouts  1.27 us (6%)
  between operations  0.64 us (3%)
    pallas_call x1, Pallas kernels, local(): pl.pallas_call(functools.partial(kernel, n_row, n_col), out_shape=(pltpu....  20.6 us
    unnamed x2, local copies, waits for them, and re-layouts  1.27 us

profile of v3, /device:TPU:0, one launch (start us, length us, event | category | flops | bytes accessed | tf_op | source)
XLA Modules:
  0.0 22.5 jit_solution(15115404943625828961)
XLA Ops:
  0.6 20.6 %residual_restrict.1 = (f32[8,32,128]{2,1,0:T(8,128)S(1)}, f32[2,32,128]{2,1,0:T(8,128)S(1)}) custom-call(s32[2,8]{1,0:T(2,128)} %bitcast.2, s32[1,8]{1,0:T(1,128)} %bitcast.3, s32[2]{0:T(128)} %aggregate_hbm.1, f32[8,2,128,128]{3,2,1,0:T(8,128)} %matrix.1, f32[2,32,128]{2,1,0:T(8,128)} %guess.1, f32[2,32,128]{2,1,0:T(8,128)} %right_side.1, ...), custom_call_target="tpu_custom_call" | custom-call | tf_op jit(solution)/shard_map/residual_restrict/pallas_call | solution.py:248
  21.2 0.7 %copy.11 = f32[8,32,128]{2,1,0:T(8,128)} copy(f32[8,32,128]{2,1,0:T(8,128)S(1)} %get-tuple-element.2) | data formatting | bytes 262144
  21.9 0.6 %copy.12 = f32[2,32,128]{2,1,0:T(8,128)} copy(f32[2,32,128]{2,1,0:T(8,128)S(1)} %get-tuple-element.3) | data formatting | bytes 65536

commit v4 on v3

--- a/solution.py
+++ b/solution.py
@@ -235,6 +235,17 @@
     pltpu.make_async_copy(sq_in, sq_in, qsend).wait()
 
 
+def store(coarse, residual, coarse_out, residual_out, sem):
+    copies = [
+        pltpu.make_async_copy(coarse, coarse_out, sem.at[0]),
+        pltpu.make_async_copy(residual, residual_out, sem.at[1]),
+    ]
+    for c in copies:
+        c.start()
+    for c in copies:
+        c.wait()
+
+
 def local(n_row, n_col, matrix, columns, counts, fine_guess, right_side, aggregate, restrict):
     blocks, nv, bs = fine_guess.shape
     rows, slots = matrix.shape[:2]
@@ -245,7 +256,7 @@
     dma = pltpu.SemaphoreType.DMA
     vmem = pl.BlockSpec(memory_space=pltpu.VMEM)
     hbm = pl.BlockSpec(memory_space=pl.ANY)
-    return pl.pallas_call(
+    coarse, residual = pl.pallas_call(
         functools.partial(kernel, n_row, n_col),
         out_shape=(
             pltpu.VMEM((NC_GRP, nv, cw), F32),
@@ -282,6 +293,16 @@
         compiler_params=pltpu.CompilerParams(collective_id=0, has_side_effects=True),
         name="residual_restrict",
     )(columns.T, counts.T, aggregate, matrix, fine_guess, right_side, restrict)
+    coarse = pltpu.with_memory_space_constraint(coarse, pltpu.VMEM)
+    residual = pltpu.with_memory_space_constraint(residual, pltpu.VMEM)
+    return pl.pallas_call(
+        store,
+        out_shape=(jax.ShapeDtypeStruct(coarse.shape, F32), jax.ShapeDtypeStruct(residual.shape, F32)),
+        in_specs=[vmem, vmem],
+        out_specs=(hbm, hbm),
+        scratch_shapes=[dma((2,))],
+        name="store",
+    )(coarse, residual)
 
 
 def solution(mesh):

time: 22.6 us -> 22 us (0.973)
  local copies, waits for them, and re-layouts: 1.27 us -> 0 us
  Pallas kernels: 20.6 us -> 21.2 us
    unnamed x2 -> x0, local copies, waits for them, and re-layouts: 1.27 us -> none
    pallas_call x0 -> x1, Pallas kernels: none -> 0.68 us  [local(): pl.pallas_call(store, out_shape=(jax.ShapeDtypeStruct(coarse.shape, F32),...]
where the time goes in v4:
time: 22 us; the launch traced here: 21.9 us
  Pallas kernels  21.2 us (96%)
  between operations  0.64 us (3%)
    pallas_call x1, Pallas kernels, local(): pl.pallas_call(functools.partial(kernel, n_row, n_col), out_shape=(pltpu....  20.6 us
    pallas_call x1, Pallas kernels, local(): pl.pallas_call(store, out_shape=(jax.ShapeDtypeStruct(coarse.shape, F32),...  0.68 us

profile of v4, /device:TPU:0, one launch (start us, length us, event | category | flops | bytes accessed | tf_op | source)
XLA Modules:
  0.0 21.9 jit_solution(14773730117639049173)
XLA Ops:
  0.6 20.6 %residual_restrict.1 = (f32[8,32,128]{2,1,0:T(8,128)S(1)}, f32[2,32,128]{2,1,0:T(8,128)S(1)}) custom-call(s32[2,8]{1,0:T(2,128)} %bitcast.2, s32[1,8]{1,0:T(1,128)} %bitcast.3, s32[2]{0:T(128)} %aggregate_hbm.1, f32[8,2,128,128]{3,2,1,0:T(8,128)} %matrix.1, f32[2,32,128]{2,1,0:T(8,128)} %guess.1, f32[2,32,128]{2,1,0:T(8,128)} %right_side.1, ...), custom_call_target="tpu_custom_call" | custom-call | tf_op jit(solution)/shard_map/residual_restrict/pallas_call | solution.py:259
  21.2 0.7 %store.1 = (f32[8,32,128]{2,1,0:T(8,128)}, f32[2,32,128]{2,1,0:T(8,128)}) custom-call(f32[8,32,128]{2,1,0:T(8,128)S(1)} %get-tuple-element.4.coarse, f32[2,32,128]{2,1,0:T(8,128)S(1)} %get-tuple-element.5.residual), custom_call_target="tpu_custom_call" | custom-call | tf_op jit(solution)/shard_map/store/pallas_call | solution.py:298

commit v5 on v4

--- a/solution.py
+++ b/solution.py
@@ -88,15 +88,6 @@
         pl.semaphore_signal(barrier, inc=1, device_id=(p, col), device_id_type=pl.DeviceIdType.MESH)
     for p in c_peers:
         pl.semaphore_signal(barrier, inc=1, device_id=(row, p), device_id_type=pl.DeviceIdType.MESH)
-    for c in reversed(scalar_loads):
-        c.start()
-    mat_loads = [pltpu.make_async_copy(matrix.at[g], mbuf.at[g], mat_sem.at[g]) for g in range(matrix.shape[0])]
-    for c in mat_loads:
-        c.start()
-    load_restrict = pltpu.make_async_copy(restrict, rbuf, load_sem.at[1])
-    load_restrict.start()
-    load_rhs = pltpu.make_async_copy(right_side, rhs, load_sem.at[2])
-    load_rhs.start()
     load_guess.wait()
     pl.semaphore_wait(barrier, len(z_peers) + len(x_peers) + len(c_peers))
 
@@ -116,6 +107,15 @@
         c = remote(xbuf.at[own_slot], xbuf.at[own_slot], xsend.at[s, 0], xrecv.at[s, 0], x_peers[s], col)
         c.start()
         x_copies.append(c)
+    for c in reversed(scalar_loads):
+        c.start()
+    mat_loads = [pltpu.make_async_copy(matrix.at[g], mbuf.at[g], mat_sem.at[g]) for g in range(matrix.shape[0])]
+    for c in mat_loads:
+        c.start()
+    load_restrict = pltpu.make_async_copy(restrict, rbuf, load_sem.at[1])
+    load_restrict.start()
+    load_rhs = pltpu.make_async_copy(right_side, rhs, load_sem.at[2])
+    load_rhs.start()
     scalar_loads[2].wait()
     for i in range(own_rows):
         agg_own[i] = jnp.full((8, 128), aggregate[i], jnp.int32).astype(F32)
@@ -213,15 +213,14 @@
                 coarse_out[c] += term.reshape(nv, 128)
     for c in a_copies:
         c.wait_recv()
-    for c in c_copies:
-        c.wait_recv()
-    for c in range(NC_GRP):
-        total = coarse_out[c].reshape(nv // 8, 8, 128)
-        for k in range(len(c_peers)):
+    for k in reversed(range(len(c_peers))):
+        c_copies[k].wait_recv()
+        for c in range(NC_GRP):
+            total = coarse_out[c].reshape(nv // 8, 8, 128)
             for i in range(own_rows):
                 mask = jnp.where(agg_in[k, i] == c, 1.0, 0.0)[None]
                 total = total + mask * con_in[k, i].reshape(nv // 8, 8, 128)
-        coarse_out[c] = total.reshape(nv, 128)
+            coarse_out[c] = total.reshape(nv, 128)
 
     pltpu.make_async_copy(sq_in, sq_in, qrecv).wait()
     all_sq = own_sq + jnp.sum(sq_in[...], axis=0)

time: 22 us -> 22.1 us (level)
  no operation moved by 1% of the time
where the time goes in v5:
time: 22.1 us; the launch traced here: 21.9 us
  Pallas kernels  21.2 us (96%)
  between operations  0.64 us (3%)
    pallas_call x1, Pallas kernels, local(): pl.pallas_call(functools.partial(kernel, n_row, n_col), out_shape=(pltpu....  20.6 us
    pallas_call x1, Pallas kernels, local(): pl.pallas_call(store, out_shape=(jax.ShapeDtypeStruct(coarse.shape, F32),...  0.68 us

profile of v5, /device:TPU:0, one launch (start us, length us, event | category | flops | bytes accessed | tf_op | source)
XLA Modules:
  0.0 21.9 jit_solution(9395833441143170549)
XLA Ops:
  0.6 20.6 %residual_restrict.1 = (f32[8,32,128]{2,1,0:T(8,128)S(1)}, f32[2,32,128]{2,1,0:T(8,128)S(1)}) custom-call(s32[2,8]{1,0:T(2,128)} %bitcast.2, s32[1,8]{1,0:T(1,128)} %bitcast.3, s32[2]{0:T(128)} %aggregate_hbm.1, f32[8,2,128,128]{3,2,1,0:T(8,128)} %matrix.1, f32[2,32,128]{2,1,0:T(8,128)} %guess.1, f32[2,32,128]{2,1,0:T(8,128)} %right_side.1, ...), custom_call_target="tpu_custom_call" | custom-call | tf_op jit(solution)/shard_map/residual_restrict/pallas_call | solution.py:258
  21.2 0.7 %store.1 = (f32[8,32,128]{2,1,0:T(8,128)}, f32[2,32,128]{2,1,0:T(8,128)}) custom-call(f32[8,32,128]{2,1,0:T(8,128)S(1)} %get-tuple-element.4.coarse, f32[2,32,128]{2,1,0:T(8,128)S(1)} %get-tuple-element.5.residual), custom_call_target="tpu_custom_call" | custom-call | tf_op jit(solution)/shard_map/store/pallas_call | solution.py:297
